TPU v7x, 32 devices: a whole 2x2x4 slice. The times are simulated.
32 devices in a mesh: fsdp: 8 (over z, x), dp: 4 (over y, core).
Axes of the slice: x: 2, y: 2, z: 4, core: 2. Of those that a mesh axis runs over, the one named last changes fastest.
Arguments:
- features: bfloat16 [8192, 1024], P(('fsdp', 'dp')), may hold values from -6 to 6
- normed: bfloat16 [8192, 4096], P(('fsdp', 'dp')), may hold values from -6 to 6
- relu_mask: int32 [8192, 4096], P(('fsdp', 'dp')), may hold values 0 or 1
- cotangent: bfloat16 [8192, 4096], P(('fsdp', 'dp')), may hold values from -40 to 40
- weight_shard: bfloat16 [1024, 4096], P('fsdp'), may hold values from -0.1875 to 0.1875
- norm_gain: float32 [4096], replicated, may hold values from 0.25 to 1.75
- inverse_deviation: float32 [4096], replicated, may hold values from 0.5 to 3
Outputs:
- grad_input: bfloat16 [8192, 1024], P(('fsdp', 'dp'))
- grad_weight: float32 [1024, 4096], P('fsdp')
- grad_gain: float32 [4096], replicated
- grad_shift: float32 [4096], replicated
All inputs are finite; a program needn't handle non-finite values. No bound on the sum of `relu_mask` on one device may be relied on, other than what follows from the above.
Results may differ from a plain program's by a relative error of at most 0.005.
Values may be sent and summed in bfloat16 or wider, within the bound.
No kernel may reach another device: no remote copies, remote signals or barrier semaphores. Data moves between devices by JAX's collectives and lax.ppermute only.
A program may use at most 128 MiB of HBM per device.

v0:
```python
import math
import jax
import jax.numpy as jnp
from jax import lax
from jax.sharding import PartitionSpec as P


def on_device(features, normed, relu_mask, cotangent, weight_shard, norm_gain, inverse_deviation):
    local_rows = features.shape[0]
    total_rows = local_rows * lax.axis_size("fsdp") * lax.axis_size("dp")
    masked = cotangent.astype(jnp.float32) * relu_mask.astype(jnp.float32)
    normed_f = normed.astype(jnp.float32)
    local_plain = jnp.sum(masked, axis=0)
    local_cross = jnp.sum(masked * normed_f, axis=0)
    sum_plain, sum_cross = lax.psum((local_plain, local_cross), ("fsdp", "dp"))
    norm_grad = (
        inverse_deviation
        * norm_gain
        * (masked - sum_plain / total_rows - normed_f * (sum_cross / total_rows))
    )
    norm_grad = norm_grad.astype(jnp.bfloat16)
    grad_input = lax.dot_general(
        norm_grad,
        lax.all_gather(weight_shard, "fsdp", axis=0, tiled=True),
        (((1,), (1,)), ((), ())),
        preferred_element_type=jnp.float32,
    ).astype(jnp.bfloat16)
    unit_block = lax.all_to_all(norm_grad, "dp", split_axis=1, concat_axis=0, tiled=True)
    unit_term = lax.dot_general(
        lax.all_gather(features, "dp", axis=0, tiled=True),
        unit_block,
        (((0,), (0,)), ((), ())),
        preferred_element_type=jnp.float32,
    )
    owner_part = lax.psum_scatter(unit_term, "fsdp", scatter_dimension=0, tiled=True)
    summed = lax.all_gather(owner_part, "dp", axis=1, tiled=True)
    rescale = 1.0 / math.sqrt(total_rows)
    return (grad_input, summed * rescale, sum_cross * rescale, sum_plain * rescale)


def solution(mesh):
    in_specs = (
        P(("fsdp", "dp"), None),
        P(("fsdp", "dp"), None),
        P(("fsdp", "dp"), None),
        P(("fsdp", "dp"), None),
        P("fsdp", None),
        P(),
        P(),
    )
    out_specs = (P(("fsdp", "dp"), None), P("fsdp", None), P(), P())
    return jax.shard_map(
        on_device, mesh=mesh, in_specs=in_specs, out_specs=out_specs, check_vma=False
    )
```

profile of v0, /device:TPU:0, one launch (start us, length us, event | category | flops | bytes accessed | tf_op | source)
XLA Modules:
  0.0 361.4 jit_solution(14963796621022647305)
XLA Ops:
  7.2 0.0 all-gather.6.cloned.1.call-start
  7.2 0.7 all-gather.6.cloned.1.call-update
  7.9 0.0 reduce-scatter.2.cloned.1.call-start
  7.9 3.3 copy.15
  11.2 5.6 %copy.14 = s32[256,4096]{0,1:T(8,128)} copy(s32[256,4096]{1,0:T(8,128)} %param.9) | data formatting | bytes 8388608 | tf_op args[2]
  16.8 4.1 %copy.13 = bf16[256,4096]{0,1:T(8,128)(2,1)} copy(bf16[256,4096]{1,0:T(8,128)(2,1)} %param.10) | data formatting | bytes 4194304 | tf_op args[3]
  21.0 0.0 copy-start.2
  21.0 0.0 copy-start.3
  21.0 4.1 %fusion.4 = (f32[4096]{0:T(1024)S(1)}, f32[4096]{0:T(1024)S(1)}) fusion(s32[256,4096]{0,1:T(8,128)} %copy.14, bf16[256,4096]{0,1:T(8,128)(2,1)} %copy.13, bf16[256,4096]{0,1:T(8,128)(2,1)S(1)} %copy.15), kind=kLoop, calls=%fused_computation.8 | loop fusion | flops 7331840 | bytes 8421376 | tf_op jit(solution)/shard_map/reduce_sum | solution.py:13
  25.1 0.0 copy-done.2
  25.1 0.0 copy-done.3
  25.1 42.3 %all-reduce = (f32[4096]{0:T(1024)S(1)}, f32[4096]{0:T(1024)S(1)}) all-reduce(f32[4096]{0:T(1024)S(1)} %get-tuple-element.17, f32[4096]{0:T(1024)S(1)} %get-tuple-element.16), channel_id=1, replica_groups=mesh['fsdp'=8,'dp'=4] {'fsdp','dp'}, use_global_device_ids=true, to_apply=%region_3.0 | all-reduce | flops 8192 | bytes 65536 | tf_op jit(solution)/shard_map/psum | solution.py:15
  67.4 0.6 broadcast_multiply_fusion.1
  68.0 4.3 %fusion.3 = bf16[256,4096]{0,1:T(8,128)(2,1)S(1)} fusion(bf16[256,4096]{0,1:T(8,128)(2,1)S(1)} %copy.15, f32[4096]{0:T(1024)S(1)} %get-tuple-element.24, f32[4096]{0:T(1024)S(1)} %get-tuple-element.21, f32[4096]{0:T(1024)S(1)} %mul.37, s32[256,4096]{0,1:T(8,128)} %copy.14, bf16[256,4096]{0,1:T(8,128)(2,1)} %copy.13), kind=kLoop, calls=%fused_computation.5 | loop fusion | flops 9437184 | bytes 10534912 | tf_op jit(solution)/shard_map/convert_element_type | solution.py:21
  72.3 0.0 copy-start
  72.3 29.0 %all_to_all.19 = bf16[256,4,1024]{0,2,1:T(8,128)(2,1)S(1)} all-to-all(bf16[256,4,1024]{0,2,1:T(8,128)(2,1)S(1)} %bitcast.9), channel_id=1, replica_groups=mesh['fsdp'=8,'dp'=4] {'dp'}, dimensions={1} | all-to-all | bytes 4194304 | tf_op jit(solution)/shard_map/all_to_all | solution.py:28
  101.3 0.0 copy-done
  101.3 2.4 copy.16
  103.7 0.0 all-gather.6.cloned.1.call-done
  103.7 6.5 %convolution_bitcast_fusion = f32[1024,1024]{0,1:T(8,128)} fusion(bf16[1024,1024]{1,0:T(8,128)(2,1)} %bitcast.11, bf16[1024,1024]{1,0:T(8,128)(2,1)} %all-gather.6.cloned.1.call-done), kind=kOutput, calls=%fused_computation.7 | convolution fusion | flops 2147483648 | bytes 8388608 | tf_op jit(solution)/shard_map/dot_general | solution.py:29
  110.3 0.0 reduce-scatter.2.cloned.1.call-update
  110.3 0.0 all-gather.8.cloned.1.call-start
  110.3 87.7 %reduce-scatter.2.cloned.1.call-done = f32[128,1024]{0,1:T(8,128)} async-done(((f32[1024,1024]{0,1:T(8,128)}), f32[128,1024]{0,1:T(8,128)}) %reduce-scatter.2.cloned.1.call-update) | async-done | bytes 524304 | tf_op jit(solution)/shard_map/reduce_scatter | solution.py:35
  198.0 0.0 all-gather.8.cloned.1.call-update
  198.1 0.0 all-gather.4.cloned.1.call-start
  198.1 0.5 all-gather.4.cloned.1.call-update
  198.6 23.2 %all-gather.8.cloned.1.call-done = f32[128,4096]{0,1:T(8,128)} async-done(((f32[128,1024]{0,1:T(8,128)}), f32[128,4096]{0,1:T(8,128)}) %all-gather.8.cloned.1.call-update) | async-done | bytes 2097168 | tf_op jit(solution)/shard_map/all_gather | solution.py:36
  221.8 3.1 broadcast_multiply_fusion
  224.9 3.0 copy.17
  227.9 120.4 %all-gather.4.cloned.1.call-done = bf16[1024,4096]{1,0:T(8,128)(2,1)} async-done(((bf16[128,4096]{1,0:T(8,128)(2,1)}), bf16[1024,4096]{1,0:T(8,128)(2,1)}) %all-gather.4.cloned.1.call-update) | async-done | bytes 8388624 | tf_op jit(solution)/shard_map/all_gather | solution.py:24
  348.3 0.0 copy-done.1
  348.3 6.6 %convolution_convert_fusion = bf16[256,1024]{1,0:T(8,128)(2,1)} fusion(bf16[256,4096]{0,1:T(8,128)(2,1)S(1)} %copy-done.1, bf16[1024,4096]{1,0:T(8,128)(2,1)} %all-gather.4.cloned.1.call-done), kind=kOutput, calls=%fused_computation.9 | convolution fusion | flops 2147745792 | bytes 11010048 | tf_op jit(solution)/shard_map/dot_general | solution.py:22
  (2 shorter events, 0.0 us)
Async XLA Ops:
  7.2 96.6 %all-gather.6.cloned.1.call-start = ((), (), s32[]{:S(2)}) async-start(), calls=%async_computation.3 | async-start | bytes 2621440 | tf_op jit(solution)/shard_map/all_gather | solution.py:30
  7.9 190.1 %reduce-scatter.2.cloned.1.call-start = ((), (), s32[]{:S(2)}) async-start(), calls=%async_computation.4 | async-start | bytes 4718592 | tf_op jit(solution)/shard_map/reduce_scatter | solution.py:35
  21.0 4.1 %copy-start.2 = (f32[4096]{0:T(1024)S(1)}, f32[4096]{0:T(1024)}, u32[]{:S(2)}) copy-start(f32[4096]{0:T(1024)} %param.13) | copy-start | bytes 49156
  21.0 4.1 %copy-start.3 = (f32[4096]{0:T(1024)S(1)}, f32[4096]{0:T(1024)}, u32[]{:S(2)}) copy-start(f32[4096]{0:T(1024)} %param.12) | copy-start | bytes 49156
  72.3 29.0 %copy-start = (bf16[256,4096]{0,1:T(8,128)(2,1)}, bf16[256,4096]{0,1:T(8,128)(2,1)S(1)}, u32[]{:S(2)}) copy-start(bf16[256,4096]{0,1:T(8,128)(2,1)S(1)} %fusion.3) | copy-start | bytes 6291460
  110.3 111.5 %all-gather.8.cloned.1.call-start = ((), (), s32[]{:S(2)}) async-start(), calls=%async_computation.5 | async-start | bytes 2621440 | tf_op jit(solution)/shard_map/all_gather | solution.py:36
  198.1 150.2 %all-gather.4.cloned.1.call-start = ((), (), s32[]{:S(2)}) async-start(), calls=%async_computation.2 | async-start | bytes 9437184 | tf_op jit(solution)/shard_map/all_gather | solution.py:24
  224.9 123.4 %copy-start.1 = (bf16[256,4096]{0,1:T(8,128)(2,1)S(1)}, bf16[256,4096]{0,1:T(8,128)(2,1)}, u32[]{:S(2)}) copy-start(bf16[256,4096]{0,1:T(8,128)(2,1)} %copy-done) | copy-start | bytes 6291460
Sparse Core Ops, SparseCore 0:
  9.5 25.2 all-gather.5
  110.4 87.5 reduce-scatter.1
  199.6 22.1 all-gather.7
  223.8 124.4 all-gather.3
where the time goes:
time: 362 us; the launch traced here: 361 us
  waiting for transfers between devices  232 us (64%)
  blocking collectives  71.3 us (20%)
  local copies, waits for them, and re-layouts  18.4 us (5%)
  between operations  13.8 us (4%)
  matrix products  13.1 us (4%)
  other arithmetic  12.1 us (3%)
    all_gather x1, waiting for transfers between devices, on_device(): lax.all_gather(weight_shard, 'fsdp', axis=0, tiled=True)  120 us
    reduce_scatter x1, waiting for transfers between devices, on_device(): lax.psum_scatter(unit_term, 'fsdp', scatter_dimension=0, tiled=True)  87.7 us
    psum x1, blocking collectives, on_device(): sum_plain, sum_cross = lax.psum((local_plain, local_cross), ('fsdp', 'dp'))  42.3 us
    all_to_all x1, blocking collectives, on_device(): lax.all_to_all(norm_grad, 'dp', split_axis=1, concat_axis=0, tiled=True)  29 us
    all_gather x1, waiting for transfers between devices, on_device(): summed = lax.all_gather(owner_part, 'dp', axis=1, tiled=True)  23.2 us
    unnamed x12, local copies, waits for them, and re-layouts  16.1 us
  transfers between devices with their start and end apart: 4, of which 3 were waited for; matrix products, arithmetic and copies ran while one was open for 8% of the time, Pallas kernels for 0%

commit v1 on v0

--- a/solution.py
+++ b/solution.py
@@ -25,7 +25,10 @@
         (((1,), (1,)), ((), ())),
         preferred_element_type=jnp.float32,
     ).astype(jnp.bfloat16)
-    unit_block = lax.all_to_all(norm_grad, "dp", split_axis=1, concat_axis=0, tiled=True)
+    unit_block = jnp.concatenate(
+        lax.all_to_all(jnp.stack(jnp.split(norm_grad, lax.axis_size("dp"), axis=1)), "dp", 0, 0),
+        axis=0,
+    )
     unit_term = lax.dot_general(
         lax.all_gather(features, "dp", axis=0, tiled=True),
         unit_block,

time: 362 us -> 349 us (0.964)
  local copies, waits for them, and re-layouts: 18.4 us -> 3.06 us
    unnamed x12 -> x5, local copies, waits for them, and re-layouts: 16.1 us -> 2.89 us
  transfers between devices with their start and end apart: 4 -> 4, of which waited for: 3 -> 3; matrix products, arithmetic and copies ran while one was open for 8% -> 5% of each run, Pallas kernels for 0% -> 0%
where the time goes in v1:
time: 349 us; the launch traced here: 348 us
  waiting for transfers between devices  233 us (67%)
  blocking collectives  71.7 us (21%)
  between operations  13.8 us (4%)
  other arithmetic  13.1 us (4%)
  matrix products  13.1 us (4%)
    all_gather x1, waiting for transfers between devices, on_device(): lax.all_gather(weight_shard, 'fsdp', axis=0, tiled=True)  120 us
    reduce_scatter x1, waiting for transfers between devices, on_device(): lax.psum_scatter(unit_term, 'fsdp', scatter_dimension=0, tiled=True)  88.5 us
    psum x1, blocking collectives, on_device(): sum_plain, sum_cross = lax.psum((local_plain, local_cross), ('fsdp', 'dp'))  42.6 us
    all_to_all x1, blocking collectives, on_device(): lax.all_to_all(jnp.stack(jnp.split(norm_grad, lax.axis_size('dp'), axis=1...  29.1 us
    all_gather x1, waiting for transfers between devices, on_device(): summed = lax.all_gather(owner_part, 'dp', axis=1, tiled=True)  23.2 us
  transfers between devices with their start and end apart: 4, of which 3 were waited for; matrix products, arithmetic and copies ran while one was open for 5% of the time, Pallas kernels for 0%

profile of v1, /device:TPU:0, one launch (start us, length us, event | category | flops | bytes accessed | tf_op | source)
XLA Modules:
  0.0 348.4 jit_solution(628145276724356067)
XLA Ops:
  7.2 0.0 all-gather.6.cloned.1.call-start
  7.2 0.7 all-gather.6.cloned.1.call-update
  7.9 0.0 copy-start
  7.9 0.0 copy-start.1
  7.9 0.0 reduce-scatter.2.cloned.1.call-start
  8.0 4.5 %fusion.4 = (f32[4096]{0:T(1024)S(1)}, f32[4096]{0:T(1024)S(1)}) fusion(s32[256,4096]{1,0:T(8,128)} %param.9, bf16[256,4096]{1,0:T(8,128)(2,1)} %param.10, bf16[256,4096]{1,0:T(8,128)(2,1)} %param.8), kind=kLoop, calls=%fused_computation.9 | loop fusion | flops 7331840 | bytes 8421376 | tf_op jit(solution)/shard_map/reduce_sum | solution.py:13
  12.5 42.6 %all-reduce = (f32[4096]{0:T(1024)S(1)}, f32[4096]{0:T(1024)S(1)}) all-reduce(f32[4096]{0:T(1024)S(1)} %get-tuple-element.9, f32[4096]{0:T(1024)S(1)} %get-tuple-element.8), channel_id=1, replica_groups=mesh['fsdp'=8,'dp'=4] {'fsdp','dp'}, use_global_device_ids=true, to_apply=%region_3.0 | all-reduce | flops 8192 | bytes 65536 | tf_op jit(solution)/shard_map/psum | solution.py:15
  55.0 0.6 broadcast_multiply_fusion.1
  55.6 0.0 copy-done
  55.6 0.0 copy-done.1
  55.7 4.7 %fusion.3 = bf16[256,4096]{1,0:T(8,128)(2,1)S(1)} fusion(bf16[256,4096]{1,0:T(8,128)(2,1)} %param.8, f32[4096]{0:T(1024)S(1)} %get-tuple-element.20, f32[4096]{0:T(1024)S(1)} %get-tuple-element.17, f32[4096]{0:T(1024)S(1)} %mul.37, s32[256,4096]{1,0:T(8,128)} %param.9, bf16[256,4096]{1,0:T(8,128)(2,1)} %param.10), kind=kLoop, calls=%fused_computation.5 | loop fusion | flops 9437184 | bytes 10534912 | tf_op jit(solution)/shard_map/convert_element_type | solution.py:21
  60.3 0.2 slice_bitcast_fusion.3
  60.5 0.3 pad_maximum_fusion
  60.8 29.1 %all_to_all.5 = bf16[4,256,1024]{2,1,0:T(8,128)(2,1)} all-to-all(bf16[4,256,1024]{2,1,0:T(8,128)(2,1)S(1)} %pad_maximum_fusion), channel_id=1, replica_groups=mesh['fsdp'=8,'dp'=4] {'dp'}, dimensions={0} | all-to-all | bytes 4194304 | tf_op jit(solution)/shard_map/all_to_all | solution.py:29
  89.9 0.0 all-gather.6.cloned.1.call-done
  89.9 6.5 %convolution_bitcast_fusion = f32[1024,1024]{0,1:T(8,128)} fusion(bf16[1024,1024]{1,0:T(8,128)(2,1)} %bitcast.15, bf16[1024,1024]{1,0:T(8,128)(2,1)} %all-gather.6.cloned.1.call-done), kind=kOutput, calls=%fused_computation.7 | convolution fusion | flops 2147483648 | bytes 8388608 | tf_op jit(solution)/shard_map/dot_general | solution.py:32
  96.5 0.0 reduce-scatter.2.cloned.1.call-update
  96.5 0.0 all-gather.8.cloned.1.call-start
  96.5 88.5 %reduce-scatter.2.cloned.1.call-done = f32[128,1024]{0,1:T(8,128)} async-done(((f32[1024,1024]{0,1:T(8,128)}), f32[128,1024]{0,1:T(8,128)}) %reduce-scatter.2.cloned.1.call-update) | async-done | bytes 524304 | tf_op jit(solution)/shard_map/reduce_scatter | solution.py:38
  185.0 0.0 all-gather.8.cloned.1.call-update
  185.0 0.0 all-gather.4.cloned.1.call-start
  185.1 0.5 all-gather.4.cloned.1.call-update
  185.6 23.2 %all-gather.8.cloned.1.call-done = f32[128,4096]{0,1:T(8,128)} async-done(((f32[128,1024]{0,1:T(8,128)}), f32[128,4096]{0,1:T(8,128)}) %all-gather.8.cloned.1.call-update) | async-done | bytes 2097168 | tf_op jit(solution)/shard_map/all_gather | solution.py:39
  208.8 3.1 broadcast_multiply_fusion
  211.9 2.9 copy.11
  214.8 120.5 %all-gather.4.cloned.1.call-done = bf16[1024,4096]{1,0:T(8,128)(2,1)} async-done(((bf16[128,4096]{1,0:T(8,128)(2,1)}), bf16[1024,4096]{1,0:T(8,128)(2,1)}) %all-gather.4.cloned.1.call-update) | async-done | bytes 8388624 | tf_op jit(solution)/shard_map/all_gather | solution.py:24
  335.3 6.5 %convolution_convert_fusion = bf16[256,1024]{1,0:T(8,128)(2,1)} fusion(bf16[256,4096]{1,0:T(8,128)(2,1)S(1)} %fusion.3, bf16[1024,4096]{1,0:T(8,128)(2,1)} %all-gather.4.cloned.1.call-done), kind=kOutput, calls=%fused_computation.10 | convolution fusion | flops 2147745792 | bytes 11010048 | tf_op jit(solution)/shard_map/dot_general | solution.py:22
  (1 shorter events, 0.0 us)
Async XLA Ops:
  7.2 82.8 %all-gather.6.cloned.1.call-start = ((), (), s32[]{:S(2)}) async-start(), calls=%async_computation.3 | async-start | bytes 2621440 | tf_op jit(solution)/shard_map/all_gather | solution.py:33
  7.9 47.7 %copy-start = (f32[4096]{0:T(1024)S(1)}, f32[4096]{0:T(1024)}, u32[]{:S(2)}) copy-start(f32[4096]{0:T(1024)} %param.13) | copy-start | bytes 49156
  7.9 47.7 %copy-start.1 = (f32[4096]{0:T(1024)S(1)}, f32[4096]{0:T(1024)}, u32[]{:S(2)}) copy-start(f32[4096]{0:T(1024)} %param.12) | copy-start | bytes 49156
  7.9 177.1 %reduce-scatter.2.cloned.1.call-start = ((), (), s32[]{:S(2)}) async-start(), calls=%async_computation.4 | async-start | bytes 4718592 | tf_op jit(solution)/shard_map/reduce_scatter | solution.py:38
  96.5 112.3 %all-gather.8.cloned.1.call-start = ((), (), s32[]{:S(2)}) async-start(), calls=%async_computation.5 | async-start | bytes 2621440 | tf_op jit(solution)/shard_map/all_gather | solution.py:39
  185.0 150.3 %all-gather.4.cloned.1.call-start = ((), (), s32[]{:S(2)}) async-start(), calls=%async_computation.2 | async-start | bytes 9437184 | tf_op jit(solution)/shard_map/all_gather | solution.py:24
Sparse Core Ops, SparseCore 0:
  9.5 25.8 all-gather.5
  96.6 88.3 reduce-scatter.1
  186.6 22.1 all-gather.7
  210.8 124.4 all-gather.3
